TPU v7x, 32 devices: a whole 2x2x4 slice. The times are simulated.
32 devices in a mesh: tm: 4 (over y, core), lev: 8 (over z, x).
Axes of the slice: x: 2, y: 2, z: 4, core: 2. Of those that a mesh axis runs over, the one named last changes fastest.
Arguments:
- obs_cell: int32 [4, 16384], P('tm'), may hold values from 0 to 65535
- innovation: float32 [4, 64, 16384], P('tm', 'lev'), may hold values from -8 to 8
- tangent: float32 [4, 64, 128, 512], P('tm', 'lev'), may hold values from -0.45 to 0.45
- damping: float32 [4, 64, 128], P('tm'), may hold values from 0.05 to 0.95
- spread: float32 [64, 128], replicated, may hold values from 0.5 to 2
- vertical: float32 [64, 64], replicated, may hold values from -0.75 to 0.75
Outputs:
- gradient: float32 [64, 128, 2, 128], P(None, 'lev', None, 'tm')
All inputs are finite; a program needn't handle non-finite values.
Results may differ from a plain program's by a relative error of at most 0.0003.
Values sent between devices are 32-bit elements; how exact they have to be, the bound alone decides.
A program may use at most 128 MiB of HBM per device.

v0:
```python
import math

import jax
import jax.numpy as jnp
from jax import lax
from jax.sharding import PartitionSpec as P

PRECISE = lax.Precision.HIGHEST
HALF_GAMMA_LOG = 0.5 * math.log(math.pi) - math.log(2.0)


def fourier_table(lon_count, wave_count):
    longitude = jnp.arange(lon_count, dtype=jnp.int32)[:, None]
    wavenumber = jnp.arange(wave_count, dtype=jnp.int32)[None, :]
    angles = (longitude * wavenumber % lon_count).astype(jnp.float32) * (2.0 * math.pi / lon_count)
    norm_factor = math.sqrt(2.0 / lon_count)
    columns = jnp.stack([jnp.cos(angles), jnp.sin(angles)], axis=2) * norm_factor
    return columns.reshape(lon_count, 2 * wave_count)


def legendre_table(first_wave, wave_block, lat_count, wave_count):
    orders = (first_wave + jnp.arange(wave_block, dtype=jnp.int32)).astype(jnp.float32)[:, None]
    row_index = jnp.arange(lat_count, dtype=jnp.float32)
    latitude = (row_index + 0.5) * (math.pi / lat_count) - 0.5 * math.pi
    sine_lat = jnp.sin(latitude)[None, :]
    cosine = jnp.cos(latitude)[None, :]
    logdiag = (
        -0.5 * math.log(2.0)
        + 0.5
        * (
            jax.scipy.special.gammaln(orders + 1.5)
            - HALF_GAMMA_LOG
            - jax.scipy.special.gammaln(orders + 1.0)
        )
        + orders * jnp.log(cosine)
    )
    diagonal = jnp.exp(logdiag)

    def advance(state_pair, degree):
        prev_one, prev_two = state_pair
        upward = jnp.sqrt(
            jnp.maximum(4.0 * degree * degree - 1.0, 1.0)
            / jnp.maximum(degree * degree - orders * orders, 1.0)
        )
        lower = degree - 1.0
        downward = jnp.sqrt(
            jnp.maximum(lower * lower - orders * orders, 0.0)
            / jnp.maximum(4.0 * lower * lower - 1.0, 1.0)
        )
        recurred = upward * (sine_lat * prev_one - downward * prev_two)
        current = jnp.where(degree < orders, 0.0, jnp.where(degree == orders, diagonal, recurred))
        return ((current, prev_one), current)

    zero_rows = jnp.zeros((wave_block, lat_count), jnp.float32)
    degrees = jnp.arange(wave_count, dtype=jnp.float32)
    _, values = lax.scan(advance, (zero_rows, zero_rows), degrees, unroll=16)
    weight = jnp.sqrt(math.pi / lat_count * cosine)
    return values * weight[None]


def forcing_field(cell_ids, innov_rows, lat_count, lon_count):
    flat_field = jnp.zeros((innov_rows.shape[0], lat_count * lon_count), jnp.float32)
    flat_field = flat_field.at[:, cell_ids].add(innov_rows)
    return flat_field.reshape(innov_rows.shape[0], lat_count, lon_count)


def shards(obs_cell, innovation, tangent, damping, spread, vertical):
    sections = lax.axis_size("tm")
    groups = lax.axis_size("lev")
    my_section = lax.axis_index("tm")
    lev_dev = tangent.shape[1]
    lat_rows = tangent.shape[2]
    lon_cols = tangent.shape[3]
    levels = damping.shape[1]
    wave_count = damping.shape[2]
    block_waves = wave_count // groups
    fourier = fourier_table(lon_cols, wave_count)
    legendre = legendre_table(
        lax.axis_index("lev") * block_waves, block_waves, lat_rows, wave_count
    )
    forcing = forcing_field(obs_cell[0], innovation[0], lat_rows, lon_cols)
    lat_block = lat_rows // sections
    level_block = levels // sections
    stacked = jnp.stack([tangent[0], forcing], axis=0)[None]
    received = lax.all_to_all(stacked, "tm", split_axis=3, concat_axis=0, tiled=True)
    damp_every = lax.all_gather(damping, "tm", axis=0, tiled=True)
    damp_mine = lax.dynamic_slice_in_dim(damp_every, my_section * level_block, level_block, 1)

    def sweep_step(step_index, carry):
        adjoint, total = carry
        time_now = sections - 1 - step_index
        fields = lax.dynamic_index_in_dim(received, time_now, 0, keepdims=False)
        forced = adjoint + fields[1]
        coeffs = jnp.einsum("klx,xc->klc", forced, fourier, precision=PRECISE)
        by_wave = lax.all_to_all(coeffs, "lev", split_axis=2, concat_axis=0, tiled=True)
        by_level = lax.all_to_all(by_wave, "tm", split_axis=0, concat_axis=1, tiled=True)
        by_level = by_level.reshape(level_block, lat_rows, block_waves, 2)
        spectral = jnp.einsum("klmp,nml->kmpn", by_level, legendre, precision=PRECISE)
        total = total + spectral
        rates = lax.dynamic_index_in_dim(damp_mine, time_now, 0, keepdims=False)
        filtered = spectral * rates[:, None, None, :]
        synthesized = jnp.einsum("kmpn,nml->klmp", filtered, legendre, precision=PRECISE)
        synthesized = synthesized.reshape(level_block, lat_rows, 2 * block_waves)
        back_rows = lax.all_to_all(synthesized, "tm", split_axis=1, concat_axis=0, tiled=True)
        back_waves = lax.all_to_all(back_rows, "lev", split_axis=0, concat_axis=2, tiled=True)
        gridded = jnp.einsum("klc,xc->klx", back_waves, fourier, precision=PRECISE)
        adjoint = fields[0] * forced + gridded
        return (adjoint, total)

    start_state = jnp.zeros((lev_dev, lat_block, lon_cols), jnp.float32)
    start_total = jnp.zeros((level_block, block_waves, 2, wave_count), jnp.float32)
    _, total = lax.fori_loop(0, sections, sweep_step, (start_state, start_total))
    spread_rows = lax.dynamic_slice_in_dim(spread, my_section * level_block, level_block, 0)
    vertical_rows = lax.dynamic_slice_in_dim(vertical, my_section * level_block, level_block, 0)
    scaled = total * spread_rows[:, None, None, :]
    partial_grad = jnp.einsum("kj,kmpn->jmpn", vertical_rows, scaled, precision=PRECISE)
    return lax.psum_scatter(partial_grad, "tm", scatter_dimension=3, tiled=True)


def solution(mesh):
    placed = (
        P("tm", None),
        P("tm", "lev", None),
        P("tm", "lev", None, None),
        P("tm", None, None),
        P(),
        P(),
    )
    return jax.shard_map(
        shards, mesh=mesh, in_specs=placed, out_specs=P(None, "lev", None, "tm"), check_vma=False
    )
```

profile of v0, /device:TPU:0, one launch (start us, length us, event | category | flops | bytes accessed | tf_op | source)
XLA Modules:
  0.0 1015.6 jit_solution(16356142913365503621)
XLA Ops:
  7.6 5.7 copy.49
  13.3 100.8 %scatter_custom_fusion = f32[8,65536]{0,1:T(8,128)} fusion(s32[16384]{0:T(1024)S(1)} %bitcast.447, f32[16384,8]{1,0:T(8,128)} %copy.49, f32[]{:T(128)} %constant.212.clone.1), kind=kCustom, calls=%fused_computation.145 | custom fusion | flops 131072 | bytes 2097664 | tf_op jit(solution)/shard_map/scatter-add | solution.py:63
  114.1 17.7 %copy.51 = f32[1,8,128,512]{3,1,0,2:T(8,128)S(1)} copy(f32[1,8,128,512]{1,3,2,0:T(8,128)} %bitcast.434) | data formatting | bytes 4194304 | tf_op jit(solution)/shard_map/stack;reshape | solution.py:84
  131.8 4.2 copy.50
  136.0 4.2 maximum_bitcast_fusion
  140.1 4.8 all-to-all-start.4
  145.2 500.8 %while.40 = (s32[]{:T(128)}, f32[16,128]{1,0:T(8,128)S(1)}, f32[16,128]{1,0:T(8,128)S(1)}, f32[8,16,16,128]{3,2,1,0:T(8,128)}, f32[8,16]{1,0:T(8,128)S(1)}, /*in...) while((s32[]{:T(128)}, f32[16,128]{1,0:T(8,128)S(1)}, ...), condition=%wide.region_2.3_spmd.clone.clone.clone.clone, body=%wide.region_1.2_spmd.clone.clone.clone.clone.sunk | while | flops 614194 | bytes 875717 | solution.py:56
  647.9 6.5 all_gather.3
  655.6 317.7 %while.39 = (s32[]{:T(128)}, f32[8,32,512]{2,1,0:T(8,128)}, f32[16,16,2,128]{3,0,2,1:T(8,128)}, f32[4,2,8,32,512]{4,2,1,3,0:T(8,128)}, f32[512,256]{1,0:T(8,128)...) while((s32[]{:T(128)}, f32[8,32,512]{2,1,0:T(8,128)}, ...), condition=%wide.region_4.5_spmd.clone, body=%wide.region_3.4_spmd.clone.sunk | while | flops 1007616000 | bytes 24142164 | solution.py:112
  659.4 15.4 %all_to_all.204 = f32[8,1,8192]{2,1,0:T(1,128)S(1)} all-to-all(f32[8,1,8192]{2,1,0:T(1,128)S(1)} %reshape.1394), channel_id=1, replica_groups=mesh['tm'=4,'lev'=8] {'lev'}, dimensions={0} | all-to-all | bytes 524288 | tf_op jit(solution)/shard_map/while/body/eval_jaxpr/all_to_all | solution.py:95
  684.2 6.0 all-to-all-done.1
  700.5 8.4 all_to_all.205
  715.5 3.6 all-to-all-start.3
  719.1 8.6 all-to-all-done.3
  740.9 11.9 %all_to_all.204 = f32[8,1,8192]{2,1,0:T(1,128)S(1)} all-to-all(f32[8,1,8192]{2,1,0:T(1,128)S(1)} %reshape.1394), channel_id=1, replica_groups=mesh['tm'=4,'lev'=8] {'lev'}, dimensions={0} | all-to-all | bytes 524288 | tf_op jit(solution)/shard_map/while/body/eval_jaxpr/all_to_all | solution.py:95
  762.2 6.0 all-to-all-done.1
  774.0 3.4 select_add_fusion.2
  779.4 8.4 all_to_all.205
  794.4 3.6 all-to-all-start.3
  798.0 8.6 all-to-all-done.3
  820.0 11.9 %all_to_all.204 = f32[8,1,8192]{2,1,0:T(1,128)S(1)} all-to-all(f32[8,1,8192]{2,1,0:T(1,128)S(1)} %reshape.1394), channel_id=1, replica_groups=mesh['tm'=4,'lev'=8] {'lev'}, dimensions={0} | all-to-all | bytes 524288 | tf_op jit(solution)/shard_map/while/body/eval_jaxpr/all_to_all | solution.py:95
  841.3 6.0 all-to-all-done.1
  858.5 8.4 all_to_all.205
  873.5 3.6 all-to-all-start.3
  877.1 8.6 all-to-all-done.3
  899.0 11.9 %all_to_all.204 = f32[8,1,8192]{2,1,0:T(1,128)S(1)} all-to-all(f32[8,1,8192]{2,1,0:T(1,128)S(1)} %reshape.1394), channel_id=1, replica_groups=mesh['tm'=4,'lev'=8] {'lev'}, dimensions={0} | all-to-all | bytes 524288 | tf_op jit(solution)/shard_map/while/body/eval_jaxpr/all_to_all | solution.py:95
  920.3 6.0 all-to-all-done.1
  937.6 8.4 all_to_all.205
  952.6 3.6 all-to-all-start.3
  956.1 8.6 all-to-all-done.3
  973.3 5.7 fusion.59
  979.1 29.6 %reduce-scatter.2.cloned.1.call-done = f32[64,16,2,32]{0,3,2,1:T(8,128)} async-done(((f32[64,16,2,128]{0,3,2,1:T(8,128)}), f32[64,16,2,32]{0,3,2,1:T(8,128)}) %reduce-scatter.2.cloned.1.call-update) | async-done | bytes 262160 | tf_op jit(solution)/shard_map/reduce_scatter | solution.py:117
  (571 shorter events, 266.6 us)
Async XLA Ops:
  6.5 966.8 %copy-start = (f32[64,64]{1,0:T(8,128)S(1)}, f32[64,64]{1,0:T(8,128)}, u32[]{:S(2)}) copy-start(f32[64,64]{1,0:T(8,128)} %param.15) | copy-start | bytes 49156
  140.1 515.4 %all-to-all-start.4 = ((f32[1,2,8,128,512]{4,2,1,0,3:T(8,128)}), f32[1,2,8,128,512]{4,2,1,0,3:T(8,128)}, u32[]{:S(2)}, u32[]{:S(2)}) async-start(f32[1,2,8,128,512]{4,2,1,0,3:T(8,128)} %maximum_bitcast_fusion), calls=%async_computation.4 | async-start | bytes 8388608 | tf_op jit(solution)/shard_map/all_to_all | solution.py:85
  145.0 863.7 %reduce-scatter.2.cloned.1.call-start = ((), (), s32[]{:S(2)}) async-start(), calls=%async_computation.6 | async-start | bytes 2621440 | tf_op jit(solution)/shard_map/reduce_scatter | solution.py:117
  646.0 1.9 copy-start.2
  646.0 9.2 copy-start.1
  680.8 9.4 all-to-all-start.1
  715.5 12.2 %all-to-all-start.3 = ((f32[8,1,8192]{2,1,0:T(1,128)}), f32[8,1,8192]{2,1,0:T(1,128)S(1)}, u32[]{:S(2)}, u32[]{:S(2)}) async-start(f32[8,1,8192]{2,1,0:T(1,128)} %reshape.1401), calls=%async_computation.3 | async-start | bytes 524288 | tf_op jit(solution)/shard_map/while/body/eval_jaxpr/all_to_all | solution.py:105
  758.8 9.4 all-to-all-start.1
  794.4 12.2 %all-to-all-start.3 = ((f32[8,1,8192]{2,1,0:T(1,128)}), f32[8,1,8192]{2,1,0:T(1,128)S(1)}, u32[]{:S(2)}, u32[]{:S(2)}) async-start(f32[8,1,8192]{2,1,0:T(1,128)} %reshape.1401), calls=%async_computation.3 | async-start | bytes 524288 | tf_op jit(solution)/shard_map/while/body/eval_jaxpr/all_to_all | solution.py:105
  837.8 9.4 all-to-all-start.1
  873.5 12.2 %all-to-all-start.3 = ((f32[8,1,8192]{2,1,0:T(1,128)}), f32[8,1,8192]{2,1,0:T(1,128)S(1)}, u32[]{:S(2)}, u32[]{:S(2)}) async-start(f32[8,1,8192]{2,1,0:T(1,128)} %reshape.1401), calls=%async_computation.3 | async-start | bytes 524288 | tf_op jit(solution)/shard_map/while/body/eval_jaxpr/all_to_all | solution.py:105
  916.9 9.4 all-to-all-start.1
  952.6 12.2 %all-to-all-start.3 = ((f32[8,1,8192]{2,1,0:T(1,128)}), f32[8,1,8192]{2,1,0:T(1,128)S(1)}, u32[]{:S(2)}, u32[]{:S(2)}) async-start(f32[8,1,8192]{2,1,0:T(1,128)} %reshape.1401), calls=%async_computation.3 | async-start | bytes 524288 | tf_op jit(solution)/shard_map/while/body/eval_jaxpr/all_to_all | solution.py:105
Sparse Core Ops, SparseCore 0:
  979.2 29.4 reduce-scatter.1
where the time goes:
time: 1030 us; the launch traced here: 1020 us
  loops' own time  396 us (38%)
  other arithmetic  224 us (22%)
  local copies, waits for them, and re-layouts  129 us (13%)
  blocking collectives  91.1 us (9%)
  waiting for transfers between devices  87.9 us (9%)
  matrix products  41.4 us (4%)
  starting transfers between devices  32.9 us (3%)
  between operations  13.5 us (1%)
    another operation x1, loops' own time, legendre_table(): _, values = lax.scan(advance, (zero_rows, zero_rows), degrees, unroll=16)  395 us
    scatter-add x1, other arithmetic, forcing_field(): flat_field = flat_field.at[:, cell_ids].add(innov_rows)  101 us
    eq x128, other arithmetic, advance(): degree == orders  79.5 us
    all_to_all x4, blocking collectives, sweep_step(): lax.all_to_all(coeffs, 'lev', split_axis=2, concat_axis=0, tiled=True)  51 us
    all_to_all x4, waiting for transfers between devices, sweep_step(): lax.all_to_all(back_rows, 'lev', split_axis=0, concat_axis=2, tiled=True)  34.5 us
    all_to_all x4, blocking collectives, sweep_step(): lax.all_to_all(synthesized, 'tm', split_axis=1, concat_axis=0, tiled=True)  33.6 us
    reduce_scatter x1, waiting for transfers between devices, shards(): return lax.psum_scatter(partial_grad, 'tm', scatter_dimension=3, tiled=True)  29.6 us
    all_to_all x4, waiting for transfers between devices, sweep_step(): lax.all_to_all(by_wave, 'tm', split_axis=0, concat_axis=1, tiled=True)  23.8 us
  transfers between devices with their start and end apart: 10, of which 9 were waited for; matrix products, arithmetic and copies ran while one was open for 11% of the time, Pallas kernels for 0%

commit v1 on v0

v1 whole, which is shorter than its diff:
```python
import functools
import math

import jax
import jax.numpy as jnp
import numpy as np
from jax import lax
from jax.experimental import pallas as pl
from jax.experimental.pallas import tpu as pltpu
from jax.sharding import PartitionSpec as P

PRECISE = lax.Precision.HIGHEST
BF16 = jnp.bfloat16
F32 = jnp.float32
NT = (((1,), (1,)), ((), ()))
NN = (((1,), (0,)), ((), ()))
VMEM_BYTES = 62 * 1024 * 1024


def dot(left, right, dims):
    return lax.dot_general(left, right, dims, preferred_element_type=F32)


def halves(value):
    high = value.astype(BF16)
    return high, (value - high.astype(F32)).astype(BF16)


def fourier_rows(lon_count, wave_count):
    index = np.arange(wave_count)[:, None] * np.arange(lon_count)[None, :] % lon_count
    angles = 2.0 * np.pi * index / lon_count
    return (np.concatenate([np.cos(angles), np.sin(angles)], 0) * np.sqrt(2.0 / lon_count)).astype(np.float32)


def legendre_coefficients(lat_count, wave_count):
    phi = (np.arange(lat_count) + 0.5) * np.pi / lat_count - 0.5 * np.pi
    orders = np.arange(wave_count).astype(np.float64)
    lead = np.array(
        [
            -0.5 * math.log(2.0)
            + 0.5 * (math.lgamma(m + 1.5) - math.lgamma(1.5) - math.lgamma(m + 1.0))
            for m in range(wave_count)
        ]
    )
    weight = np.sqrt(np.pi * np.cos(phi) / lat_count)
    diagonal = weight[:, None] * np.exp(lead[None, :] + orders[None, :] * np.log(np.cos(phi))[:, None])
    mu = np.broadcast_to(np.sin(phi)[:, None], (lat_count, wave_count))
    degree = orders[:, None]
    above = degree > orders[None, :]
    gap = np.where(above, degree**2 - orders[None, :] ** 2, 1.0)
    up = np.where(above, np.sqrt(np.maximum(4.0 * degree**2 - 1.0, 0.0) / gap), 0.0)
    lower = degree - 1.0
    down = np.sqrt(np.maximum(lower**2 - orders[None, :] ** 2, 0.0) / np.maximum(4.0 * lower**2 - 1.0, 1.0))
    both = up * down
    return [np.asarray(a, np.float32) for a in (mu, diagonal, up, both)]


def forcing_kernel(lat_rows, lon_cols, cell_ref, innov_ref, out_ref):
    cells = cell_ref[0]
    width = cells.shape[1]
    rows = cells // lon_cols
    cols = cells - rows * lon_cols
    innov = innov_ref[0]
    levels = innov.shape[0]
    hit = lax.broadcasted_iota(jnp.int32, (lat_rows, width), 0) == rows
    spread_cols = jnp.where(
        lax.broadcasted_iota(jnp.int32, (lon_cols, width), 0) == cols, 1.0, 0.0
    ).astype(BF16)
    high = innov.astype(BF16).astype(F32)
    low = innov - high
    pieces = [jnp.where(hit, part[k : k + 1, :], 0.0).astype(BF16) for part in (high, low) for k in range(levels)]
    field = dot(jnp.concatenate(pieces, 0), spread_cols, NT)
    field = field[: levels * lat_rows] + field[levels * lat_rows :]

    @pl.when(pl.program_id(1) == 0)
    def _():
        out_ref[0] = field

    @pl.when(pl.program_id(1) > 0)
    def _():
        out_ref[0] += field


def forcing_fields(cells, innov, lat_rows, lon_cols):
    times, levels, count = innov.shape
    width = math.gcd(count, 2048)
    body = functools.partial(forcing_kernel, lat_rows, lon_cols)
    return pl.pallas_call(
        body,
        grid=(times, count // width),
        in_specs=[
            pl.BlockSpec((1, 1, width), lambda t, c: (t, 0, c)),
            pl.BlockSpec((1, levels, width), lambda t, c: (t, 0, c)),
        ],
        out_specs=pl.BlockSpec((1, levels * lat_rows, lon_cols), lambda t, c: (t, 0, 0)),
        out_shape=jax.ShapeDtypeStruct((times, levels * lat_rows, lon_cols), F32),
        compiler_params=pltpu.CompilerParams(vmem_limit_bytes=VMEM_BYTES),
        cost_estimate=pl.CostEstimate(
            flops=4 * times * levels * lat_rows * lon_cols * count, bytes_accessed=8 * 2**20, transcendentals=0
        ),
    )(cells.reshape(times, 1, count), innov)


def sweep_kernel(
    field_ref, tangent_ref, damp_ref, fhigh_ref, flow_ref, mu_ref, diag_ref, up_ref, both_ref,
    total_ref, table, high, low, packed, adjoint,
):
    times, rows, lon_cols = field_ref.shape
    lat_rows, waves = mu_ref.shape
    levels = rows // lat_rows
    group = damp_ref.shape[1]
    half = group // 2

    orders = lax.broadcasted_iota(jnp.int32, (lat_rows, waves), 1)

    def advance(n, state):
        one, two = state
        recurred = up_ref[pl.ds(n, 1), :] * (mu_ref[...] * one) - both_ref[pl.ds(n, 1), :] * two
        value = jnp.where(orders == n, diag_ref[...], recurred)
        table[pl.ds(n, waves, stride=waves), :] = value.T
        return value, one

    zero = 0.0 * mu_ref[...]
    lax.fori_loop(0, waves, advance, (zero, zero))

    def split(m, carry):
        upper, lower = halves(table[pl.ds(m * waves, waves), :])
        high[m] = upper
        low[m] = lower
        return carry

    lax.fori_loop(0, waves, split, 0, unroll=2)

    def pair_sum(value):
        return value + pltpu.roll(value, half, 0)

    in_high = lax.broadcasted_iota(jnp.int32, (group, waves), 0) < half
    adjoint[...] = jnp.zeros_like(adjoint)
    total_ref[...] = jnp.zeros_like(total_ref)

    def analyse(t):
        forced = adjoint[...] + field_ref[t]
        adjoint[...] = forced
        for k in range(levels):
            upper, lower = halves(forced[k * lat_rows : (k + 1) * lat_rows])
            coeffs = (
                dot(fhigh_ref[...], upper, NT) + dot(flow_ref[...], upper, NT) + dot(fhigh_ref[...], lower, NT)
            )
            for p in range(2):
                part = coeffs[p * waves : (p + 1) * waves]
                rounded = part.astype(BF16).astype(F32)
                packed[pl.ds(2 * k + p, waves, stride=group), :] = rounded
                packed[pl.ds(half + 2 * k + p, waves, stride=group), :] = part - rounded

    def spectral_of(m):
        left = packed[pl.ds(pl.multiple_of(m * group, group), group), :].astype(BF16)
        value = pair_sum(dot(left, high[m], NT) + dot(left, low[m], NT))
        total_ref[m] += value
        return value

    def step(s, carry):
        t = times - 1 - s
        analyse(t)
        damp = damp_ref[t]

        def wave(m, inner):
            filtered = spectral_of(m) * damp
            rounded = filtered.astype(BF16).astype(F32)
            left = jnp.where(in_high, rounded, filtered - rounded).astype(BF16)
            back = pair_sum(dot(left, high[m], NN) + dot(left, low[m], NN))
            packed[pl.ds(pl.multiple_of(m * group, group), group), :] = back
            return inner

        lax.fori_loop(0, waves, wave, 0, unroll=8)
        for k in range(levels):
            synth = jnp.concatenate(
                [packed[pl.ds(2 * k + p, waves, stride=group), :] for p in range(2)], 0
            ).T
            upper, lower = halves(synth)
            gridded = dot(upper, fhigh_ref[...], NN) + dot(lower, fhigh_ref[...], NN) + dot(upper, flow_ref[...], NN)
            place = pl.ds(k * lat_rows, lat_rows)
            adjoint[place, :] = tangent_ref[t, place, :] * adjoint[place, :] + gridded
        return carry

    lax.fori_loop(0, times - 1, step, 0)
    analyse(0)

    def last(m, inner):
        spectral_of(m)
        return inner

    lax.fori_loop(0, waves, last, 0, unroll=8)


def sweep(fields, tangent, damp, lat_rows, waves):
    times, rows, lon_cols = fields.shape
    group = damp.shape[1]
    fourier = fourier_rows(lon_cols, waves)
    fhigh = fourier.astype(jnp.bfloat16)
    flow = (fourier - fhigh.astype(np.float32)).astype(jnp.bfloat16)
    mu, diagonal, up, both = legendre_coefficients(lat_rows, waves)
    return pl.pallas_call(
        sweep_kernel,
        in_specs=[pl.BlockSpec(memory_space=pltpu.VMEM)] * 9,
        out_specs=pl.BlockSpec(memory_space=pltpu.VMEM),
        out_shape=jax.ShapeDtypeStruct((waves, group, waves), F32),
        scratch_shapes=[
            pltpu.VMEM((waves * waves, lat_rows), F32),
            pltpu.VMEM((waves, waves, lat_rows), BF16),
            pltpu.VMEM((waves, waves, lat_rows), BF16),
            pltpu.VMEM((waves * group, lat_rows), F32),
            pltpu.VMEM((rows, lon_cols), F32),
        ],
        compiler_params=pltpu.CompilerParams(vmem_limit_bytes=VMEM_BYTES),
    )(fields, tangent, damp, fhigh, flow, mu, diagonal, up, both)


def shards(obs_cell, innovation, tangent, damping, spread, vertical):
    sections = lax.axis_size("tm")
    groups = lax.axis_size("lev")
    me_tm = lax.axis_index("tm")
    me_lev = lax.axis_index("lev")
    lev_dev, lat_rows, lon_cols = tangent.shape[1:]
    levels, waves = damping.shape[1:]
    mine = -(-lev_dev // sections)
    mine += mine % 2
    padded = mine * sections

    def pad_levels(value, axis):
        widths = [(0, 0)] * value.ndim
        widths[axis] = (0, padded - value.shape[axis])
        return jnp.pad(value, widths) if padded > value.shape[axis] else value

    innov = lax.all_to_all(
        pad_levels(innovation[0], 0).reshape(sections, mine, -1), "tm", split_axis=0, concat_axis=0, tiled=True
    )
    cells = lax.all_gather(obs_cell, "tm", axis=0, tiled=True)
    damp_every = lax.all_gather(damping, "tm", axis=0, tiled=True)
    rates = lax.all_to_all(
        pad_levels(tangent[0], 0).reshape(sections, mine * lat_rows, lon_cols),
        "tm", split_axis=0, concat_axis=0, tiled=True,
    )
    fields = forcing_fields(cells, innov, lat_rows, lon_cols)
    damp_block = pad_levels(lax.dynamic_slice_in_dim(damp_every, me_lev * lev_dev, lev_dev, 1), 1)
    damp_mine = lax.dynamic_slice_in_dim(damp_block, me_tm * mine, mine, 1)
    damp_rows = jnp.tile(jnp.repeat(damp_mine, 2, axis=1), (1, 2, 1))
    total = sweep(fields, rates, damp_rows, lat_rows, waves)

    block_m = waves // groups
    block_n = waves // sections
    outgoing = total[:, : 2 * mine].reshape(groups, block_m, mine, 2, sections, block_n)
    outgoing = outgoing.transpose(0, 4, 2, 1, 3, 5).reshape(groups * sections, mine, block_m * 2 * block_n)
    arrived = lax.all_to_all(outgoing, ("lev", "tm"), split_axis=0, concat_axis=0, tiled=True)
    arrived = arrived.reshape(groups, padded, block_m * 2, block_n)[:, :lev_dev]
    arrived = arrived.reshape(levels, block_m * 2, block_n)
    spread_cols = lax.dynamic_slice_in_dim(spread, me_tm * block_n, block_n, 1)
    scaled = (arrived * spread_cols[:, None, :]).reshape(levels, block_m * 2 * block_n)
    result = jnp.einsum("kj,kx->jx", vertical, scaled, precision=PRECISE)
    return result.reshape(levels, block_m, 2, block_n)


def solution(mesh):
    placed = (
        P("tm", None),
        P("tm", "lev", None),
        P("tm", "lev", None, None),
        P("tm", None, None),
        P(),
        P(),
    )
    return jax.shard_map(
        shards, mesh=mesh, in_specs=placed, out_specs=P(None, "lev", None, "tm"), check_vma=False
    )
```

time: 1030 us -> 216 us (0.21); the launches traced: 1020 us -> 215 us
  loops' own time: 396 us -> 0 us
  other arithmetic: 224 us -> 0 us
  Pallas kernels: 0 us -> 163 us
  local copies, waits for them, and re-layouts: 129 us -> 9.54 us
  waiting for transfers between devices: 87.9 us -> 10.2 us
  blocking collectives: 91.1 us -> 16.6 us
  matrix products: 41.4 us -> 0.42 us
  starting transfers between devices: 32.9 us -> 15.7 us
  between operations: 13.5 us -> 0.12 us
    another operation x2 -> x0, loops' own time: 396 us -> none  [the longest x1 395 us: legendre_table(): _, values = lax.scan(advance, (zero_rows, zero_rows), degrees, unroll=16)]
    pallas_call x0 -> x2, Pallas kernels: none -> 163 us  [the longest x1 117 us: sweep(): pl.pallas_call(sweep_kernel, in_specs=[pl.BlockSpec(memory_space=pltpu.VM...]
    scatter-add x1 -> x0, other arithmetic: 101 us -> none  [forcing_field(): flat_field = flat_field.at[:, cell_ids].add(innov_rows)]
    all_to_all x8 -> x0, blocking collectives: 84.6 us -> none  [the longest x4 51 us: sweep_step(): lax.all_to_all(coeffs, 'lev', split_axis=2, concat_axis=0, tiled=True)]
    eq x128 -> x0, other arithmetic: 79.5 us -> none  [advance(): degree == orders]
    all_to_all x9 -> x3, waiting for transfers between devices: 58.3 us -> 10.2 us  [the longest x1 10.2 us: shards(): lax.all_to_all(outgoing, ('lev', 'tm'), split_axis=0, concat_axis=0, tile...]
    all_to_all x40 -> x0, local copies, waits for them, and re-layouts: 46.8 us -> none  [the longest x12 15 us: sweep_step(): lax.all_to_all(back_rows, 'lev', split_axis=0, concat_axis=2, tiled=True)]
    dot_general x17 -> x1, matrix products: 41.4 us -> 0.42 us  [shards(): result = jnp.einsum('kj,kx->jx', vertical, scaled, precision=PRECISE)]
  transfers between devices with their start and end apart: 10 -> 3, of which waited for: 9 -> 1; matrix products, arithmetic and copies ran while one was open for 11% -> 0% of each run, Pallas kernels for 0% -> 21%
where the time goes in v1:
time: 216 us; the launch traced here: 215 us
  Pallas kernels  163 us (75%)
  blocking collectives  16.6 us (8%)
  starting transfers between devices  15.7 us (7%)
  waiting for transfers between devices  10.2 us (5%)
  local copies, waits for them, and re-layouts  9.54 us (4%)
    pallas_call x1, Pallas kernels, sweep(): pl.pallas_call(sweep_kernel, in_specs=[pl.BlockSpec(memory_space=pltpu.VM...  117 us
    pallas_call x1, Pallas kernels, forcing_fields(): pl.pallas_call(body, grid=(times, count // width), in_specs=[pl.BlockSpec...  45.6 us
    all_gather x1, blocking collectives, shards(): damp_every = lax.all_gather(damping, 'tm', axis=0, tiled=True)  10.3 us
    all_to_all x1, waiting for transfers between devices, shards(): lax.all_to_all(outgoing, ('lev', 'tm'), split_axis=0, concat_axis=0, tile...  10.2 us
    all_to_all x1, starting transfers between devices, shards(): lax.all_to_all(outgoing, ('lev', 'tm'), split_axis=0, concat_axis=0, tile...  6.94 us
    all_gather x1, blocking collectives, shards(): cells = lax.all_gather(obs_cell, 'tm', axis=0, tiled=True)  6.28 us
    all_to_all x1, starting transfers between devices, shards(): lax.all_to_all(pad_levels(tangent[0], 0).reshape(sections, mine * lat_row...  4.45 us
  transfers between devices with their start and end apart: 3, of which 1 were waited for; matrix products, arithmetic and copies ran while one was open for 0% of the time, Pallas kernels for 21%

profile of v1, /device:TPU:0, one launch (start us, length us, event | category | flops | bytes accessed | tf_op | source)
XLA Modules:
  0.0 215.3 jit_solution(14618976614000531179)
XLA Ops:
  0.0 0.0 copy-start
  0.0 2.2 %reshape_squeeze.6 = f32[4,2,16384]{2,1,0:T(2,128)} reshape(f32[1,8,16384]{2,1,0:T(8,128)} %param.13) | data formatting | bytes 1048576 | tf_op jit(solution)/shard_map/reshape;squeeze | solution.py:235
  2.2 4.3 %all-to-all-start = ((f32[4,2,16384]{2,1,0:T(2,128)}), f32[4,2,16384]{2,1,0:T(2,128)S(1)}, u32[]{:S(2)}, u32[]{:S(2)}) async-start(f32[4,2,16384]{2,1,0:T(2,128)} %reshape_squeeze.6), calls=%async_computation | async-start | bytes 1048576 | tf_op jit(solution)/shard_map/all_to_all | solution.py:234
  6.4 0.0 copy-done.3
  6.5 10.3 %all_gather.7 = f32[4,64,128]{2,1,0:T(8,128)S(1)} all-gather(f32[1,64,128]{2,1,0:T(8,128)S(1)} %copy-done.3), channel_id=1, replica_groups=mesh['tm'=4,'lev'=8] {'tm'}, dimensions={0}, use_global_device_ids=true | all-gather | bytes 163840 | tf_op jit(solution)/shard_map/all_gather | solution.py:238
  16.8 0.0 copy-done.2
  16.8 6.3 %all-gather.cell_ref = s32[4,1,16384]{2,1,0:T(1,128)} all-gather(s32[1,1,16384]{2,1,0:T(1,128)S(1)} %bitcast.17), channel_id=1, replica_groups=mesh['tm'=4,'lev'=8] {'tm'}, dimensions={0}, use_global_device_ids=true | all-gather | bytes 327680 | tf_op jit(solution)/shard_map/all_gather | solution.py:237
  23.1 0.0 all-to-all-done.innov_ref
  23.1 0.0 copy-start.1
  23.1 0.8 copy-done.1
  23.9 4.4 %all-to-all-start.1 = ((f32[4,256,512]{2,1,0:T(8,128)}), f32[4,256,512]{2,1,0:T(8,128)}, u32[]{:S(2)}, u32[]{:S(2)}) async-start(f32[4,256,512]{2,1,0:T(8,128)} %bitcast.1), calls=%async_computation.1 | async-start | bytes 4194304 | tf_op jit(solution)/shard_map/all_to_all | solution.py:239
  28.4 45.6 %shard_map.118.field_ref = f32[4,256,512]{2,1,0:T(8,128)} custom-call(s32[4,1,16384]{2,1,0:T(1,128)} %all-gather.cell_ref, f32[4,2,16384]{2,1,0:T(2,128)} %copy-done.1), custom_call_target="tpu_custom_call" | custom-call | flops 34359738368 | bytes 8388608 | tf_op jit(solution)/shard_map/pallas_call | solution.py:88
  73.9 0.0 all-to-all-done.1.tangent_ref
  73.9 0.6 tile.11
  74.5 117.2 %shard_map.119 = f32[128,8,128]{2,1,0:T(8,128)} custom-call(f32[4,256,512]{2,1,0:T(8,128)} %shard_map.118.field_ref, f32[4,256,512]{2,1,0:T(8,128)} %all-to-all-done.1.tangent_ref, f32[4,8,128]{2,1,0:T(8,128)} %bitcast.16, bf16[256,512]{1,0:T(8,128)(2,1)} %constant.47.clone.fhigh_ref, bf16[256,512]{1,0:T(8,128)(2,1)} %constant.48.clone.flow_ref, ...), custom_call_target="tpu_custom_call" | custom-call | tf_op jit(solution)/shard_map/pallas_call | solution.py:202
  191.7 1.1 slice.4
  192.8 0.5 reshape.21
  193.3 0.0 copy-start.4
  193.3 0.5 copy.28
  193.9 1.4 reshape.22
  195.2 0.9 copy.23
  196.1 6.9 %all-to-all-start.2 = ((f32[32,2,1024]{2,1,0:T(2,128)}), f32[32,2,1024]{2,1,0:T(2,128)S(1)}, u32[]{:S(2)}, u32[]{:S(2)}) async-start(f32[32,2,1024]{2,1,0:T(2,128)} %copy.23), calls=%async_computation.2 | async-start | bytes 524288 | tf_op jit(solution)/shard_map/all_to_all | solution.py:253
  203.1 0.0 copy-done.4
  203.1 0.1 constant_dynamic-slice_fusion
  203.2 0.1 copy.24
  203.2 0.1 mul.23
  203.3 0.2 copy.25
  203.5 10.2 %all-to-all-done.2 = f32[32,2,1024]{2,1,0:T(2,128)S(1)} async-done(((f32[32,2,1024]{2,1,0:T(2,128)}), f32[32,2,1024]{2,1,0:T(2,128)S(1)}, u32[]{:S(2)}, u32[]{:S(2)}) %all-to-all-start.2) | async-done | bytes 262176 | tf_op jit(solution)/shard_map/all_to_all | solution.py:253
  213.6 0.2 reshape_reshape.3
  213.8 0.0 copy-done
  213.8 0.4 convolution_bitcast_fusion
  214.3 1.0 copy.26
  (4 shorter events, 0.0 us)
Async XLA Ops:
  0.0 213.8 %copy-start = (f32[64,64]{1,0:T(8,128)S(1)}, f32[64,64]{1,0:T(8,128)}, u32[]{:S(2)}) copy-start(f32[64,64]{1,0:T(8,128)} %param.17) | copy-start | bytes 49156
  0.0 6.4 %copy-start.3 = (f32[1,64,128]{2,1,0:T(8,128)S(1)}, f32[1,64,128]{2,1,0:T(8,128)}, u32[]{:S(2)}) copy-start(f32[1,64,128]{2,1,0:T(8,128)} %param.15) | copy-start | bytes 98308
  0.0 16.8 %copy-start.2 = (s32[1,16384]{1,0:T(1,128)S(1)}, s32[1,16384]{1,0:T(1,128)}, u32[]{:S(2)}) copy-start(s32[1,16384]{1,0:T(1,128)} %param.12) | copy-start | bytes 196612
  2.2 20.9 %all-to-all-start = ((f32[4,2,16384]{2,1,0:T(2,128)}), f32[4,2,16384]{2,1,0:T(2,128)S(1)}, u32[]{:S(2)}, u32[]{:S(2)}) async-start(f32[4,2,16384]{2,1,0:T(2,128)} %reshape_squeeze.6), calls=%async_computation | async-start | bytes 1048576 | tf_op jit(solution)/shard_map/all_to_all | solution.py:234
  23.1 0.8 copy-start.1
  23.9 50.0 %all-to-all-start.1 = ((f32[4,256,512]{2,1,0:T(8,128)}), f32[4,256,512]{2,1,0:T(8,128)}, u32[]{:S(2)}, u32[]{:S(2)}) async-start(f32[4,256,512]{2,1,0:T(8,128)} %bitcast.1), calls=%async_computation.1 | async-start | bytes 4194304 | tf_op jit(solution)/shard_map/all_to_all | solution.py:239
  193.3 9.8 %copy-start.4 = (f32[64,128]{1,0:T(8,128)S(1)}, f32[64,128]{1,0:T(8,128)}, u32[]{:S(2)}) copy-start(f32[64,128]{1,0:T(8,128)} %param.16) | copy-start | bytes 98308
  196.1 17.5 %all-to-all-start.2 = ((f32[32,2,1024]{2,1,0:T(2,128)}), f32[32,2,1024]{2,1,0:T(2,128)S(1)}, u32[]{:S(2)}, u32[]{:S(2)}) async-start(f32[32,2,1024]{2,1,0:T(2,128)} %copy.23), calls=%async_computation.2 | async-start | bytes 524288 | tf_op jit(solution)/shard_map/all_to_all | solution.py:253

commit v2 on v1

--- a/solution.py
+++ b/solution.py
@@ -121,7 +121,7 @@
         return value, one
 
     zero = 0.0 * mu_ref[...]
-    lax.fori_loop(0, waves, advance, (zero, zero))
+    lax.fori_loop(0, waves, advance, (zero, zero), unroll=8)
 
     def split(m, carry):
         upper, lower = halves(table[pl.ds(m * waves, waves), :])
@@ -129,7 +129,7 @@
         low[m] = lower
         return carry
 
-    lax.fori_loop(0, waves, split, 0, unroll=2)
+    lax.fori_loop(0, waves, split, 0, unroll=4)
 
     def pair_sum(value):
         return value + pltpu.roll(value, half, 0)
@@ -152,26 +152,41 @@
                 packed[pl.ds(2 * k + p, waves, stride=group), :] = rounded
                 packed[pl.ds(half + 2 * k + p, waves, stride=group), :] = part - rounded
 
-    def spectral_of(m):
-        left = packed[pl.ds(pl.multiple_of(m * group, group), group), :].astype(BF16)
-        value = pair_sum(dot(left, high[m], NT) + dot(left, low[m], NT))
-        total_ref[m] += value
-        return value
+    batch = math.gcd(waves, 16)
+
+    def lanes_of(b):
+        return pl.ds(pl.multiple_of(b * batch * group, batch * group), batch * group)
+
+    def parts_of(value):
+        return [value[u * group : (u + 1) * group] for u in range(batch)]
+
+    def product(lefts, b, dims):
+        return [
+            pair_sum(dot(left, high[b * batch + u], dims) + dot(left, low[b * batch + u], dims))
+            for u, left in enumerate(lefts)
+        ]
+
+    def spectral_of(b):
+        lefts = parts_of(packed[lanes_of(b), :].astype(BF16))
+        values = product(lefts, b, NT)
+        total_ref[lanes_of(b), :] += jnp.concatenate(values, 0)
+        return values
 
     def step(s, carry):
         t = times - 1 - s
         analyse(t)
         damp = damp_ref[t]
 
-        def wave(m, inner):
-            filtered = spectral_of(m) * damp
-            rounded = filtered.astype(BF16).astype(F32)
-            left = jnp.where(in_high, rounded, filtered - rounded).astype(BF16)
-            back = pair_sum(dot(left, high[m], NN) + dot(left, low[m], NN))
-            packed[pl.ds(pl.multiple_of(m * group, group), group), :] = back
+        def wave(b, inner):
+            lefts = []
+            for value in spectral_of(b):
+                filtered = value * damp
+                rounded = filtered.astype(BF16).astype(F32)
+                lefts.append(jnp.where(in_high, rounded, filtered - rounded).astype(BF16))
+            packed[lanes_of(b), :] = jnp.concatenate(product(lefts, b, NN), 0)
             return inner
 
-        lax.fori_loop(0, waves, wave, 0, unroll=8)
+        lax.fori_loop(0, waves // batch, wave, 0)
         for k in range(levels):
             synth = jnp.concatenate(
                 [packed[pl.ds(2 * k + p, waves, stride=group), :] for p in range(2)], 0
@@ -185,11 +200,11 @@
     lax.fori_loop(0, times - 1, step, 0)
     analyse(0)
 
-    def last(m, inner):
-        spectral_of(m)
+    def last(b, inner):
+        spectral_of(b)
         return inner
 
-    lax.fori_loop(0, waves, last, 0, unroll=8)
+    lax.fori_loop(0, waves // batch, last, 0)
 
 
 def sweep(fields, tangent, damp, lat_rows, waves):
@@ -203,7 +218,7 @@
         sweep_kernel,
         in_specs=[pl.BlockSpec(memory_space=pltpu.VMEM)] * 9,
         out_specs=pl.BlockSpec(memory_space=pltpu.VMEM),
-        out_shape=jax.ShapeDtypeStruct((waves, group, waves), F32),
+        out_shape=jax.ShapeDtypeStruct((waves * group, waves), F32),
         scratch_shapes=[
             pltpu.VMEM((waves * waves, lat_rows), F32),
             pltpu.VMEM((waves, waves, lat_rows), BF16),
@@ -231,24 +246,35 @@
         widths[axis] = (0, padded - value.shape[axis])
         return jnp.pad(value, widths) if padded > value.shape[axis] else value
 
-    innov = lax.all_to_all(
-        pad_levels(innovation[0], 0).reshape(sections, mine, -1), "tm", split_axis=0, concat_axis=0, tiled=True
-    )
-    cells = lax.all_gather(obs_cell, "tm", axis=0, tiled=True)
-    damp_every = lax.all_gather(damping, "tm", axis=0, tiled=True)
+    count = obs_cell.shape[1]
+    damp_block = pad_levels(lax.dynamic_slice_in_dim(damping[0], me_lev * lev_dev, lev_dev, 0), 0)
+    damp_block = damp_block.reshape(sections, mine * waves)
+    damp_deep = -(-mine * waves // count)
+    damp_block = jnp.pad(damp_block, ((0, 0), (0, damp_deep * count - mine * waves)))
+    message = jnp.concatenate(
+        [
+            pad_levels(innovation[0], 0).reshape(sections, mine, count),
+            jnp.broadcast_to(obs_cell.astype(F32)[None], (sections, 1, count)),
+            damp_block.reshape(sections, damp_deep, count),
+        ],
+        1,
+    )
+    message = lax.all_to_all(message, "tm", split_axis=0, concat_axis=0, tiled=True)
+    innov = message[:, :mine]
+    cells = message[:, mine].astype(jnp.int32)
+    damp_mine = message[:, mine + 1 :].reshape(sections, damp_deep * count)[:, : mine * waves]
+    damp_mine = damp_mine.reshape(sections, mine, waves)
     rates = lax.all_to_all(
         pad_levels(tangent[0], 0).reshape(sections, mine * lat_rows, lon_cols),
         "tm", split_axis=0, concat_axis=0, tiled=True,
     )
     fields = forcing_fields(cells, innov, lat_rows, lon_cols)
-    damp_block = pad_levels(lax.dynamic_slice_in_dim(damp_every, me_lev * lev_dev, lev_dev, 1), 1)
-    damp_mine = lax.dynamic_slice_in_dim(damp_block, me_tm * mine, mine, 1)
     damp_rows = jnp.tile(jnp.repeat(damp_mine, 2, axis=1), (1, 2, 1))
     total = sweep(fields, rates, damp_rows, lat_rows, waves)
 
     block_m = waves // groups
     block_n = waves // sections
-    outgoing = total[:, : 2 * mine].reshape(groups, block_m, mine, 2, sections, block_n)
+    outgoing = total.reshape(waves, 4 * mine, waves)[:, : 2 * mine].reshape(groups, block_m, mine, 2, sections, block_n)
     outgoing = outgoing.transpose(0, 4, 2, 1, 3, 5).reshape(groups * sections, mine, block_m * 2 * block_n)
     arrived = lax.all_to_all(outgoing, ("lev", "tm"), split_axis=0, concat_axis=0, tiled=True)
     arrived = arrived.reshape(groups, padded, block_m * 2, block_n)[:, :lev_dev]

time: 216 us -> 141 us (0.65)
  Pallas kernels: 163 us -> 88.3 us
  starting transfers between devices: 15.7 us -> 10.8 us
  other arithmetic: 0 us -> 2.74 us
    pallas_call x1, Pallas kernels: 117 us -> 42.7 us  [sweep(): pl.pallas_call(sweep_kernel, in_specs=[pl.BlockSpec(memory_space=pltpu.VM...]
    all_to_all x0 -> x1, blocking collectives: none -> 18.5 us  [shards(): lax.all_to_all(message, 'tm', split_axis=0, concat_axis=0, tiled=True)]
    all_gather x2 -> x0, blocking collectives: 16.6 us -> none  [the longest x1 10.3 us: shards(): damp_every = lax.all_gather(damping, 'tm', axis=0, tiled=True)]
    all_to_all x1 -> x0, starting transfers between devices: 4.27 us -> none  [shards(): lax.all_to_all(pad_levels(innovation[0], 0).reshape(sections, mine, -1),...]
  transfers between devices with their start and end apart: 3 -> 2, of which waited for: 1 -> 1; matrix products, arithmetic and copies ran while one was open for 0% -> 2% of each run, Pallas kernels for 21% -> 32%
where the time goes in v2:
time: 141 us
  Pallas kernels  88.3 us (63%)
  blocking collectives  18.5 us (13%)
  starting transfers between devices  10.8 us (8%)
  waiting for transfers between devices  10.2 us (7%)
  local copies, waits for them, and re-layouts  9.8 us (7%)
  other arithmetic  2.74 us (2%)
    pallas_call x1, Pallas kernels, forcing_fields(): pl.pallas_call(body, grid=(times, count // width), in_specs=[pl.BlockSpec...  45.5 us
    pallas_call x1, Pallas kernels, sweep(): pl.pallas_call(sweep_kernel, in_specs=[pl.BlockSpec(memory_space=pltpu.VM...  42.7 us
    all_to_all x1, blocking collectives, shards(): lax.all_to_all(message, 'tm', split_axis=0, concat_axis=0, tiled=True)  18.5 us
    all_to_all x1, waiting for transfers between devices, shards(): lax.all_to_all(outgoing, ('lev', 'tm'), split_axis=0, concat_axis=0, tile...  10.2 us
    all_to_all x1, starting transfers between devices, shards(): lax.all_to_all(outgoing, ('lev', 'tm'), split_axis=0, concat_axis=0, tile...  6.32 us
    all_to_all x1, starting transfers between devices, shards(): lax.all_to_all(pad_levels(tangent[0], 0).reshape(sections, mine * lat_row...  4.45 us
  transfers between devices with their start and end apart: 2, of which 1 were waited for; matrix products, arithmetic and copies ran while one was open for 2% of the time, Pallas kernels for 32%

profile of v2, /device:TPU:0, one launch (start us, length us, event | category | flops | bytes accessed | tf_op | source)
XLA Modules:
  0.0 140.8 jit_solution(5177221866392293401)
XLA Ops:
  0.0 0.0 copy-start
  0.0 0.7 constant_dynamic-slice_fusion.1
  0.8 0.2 reshape.39
  0.9 1.3 reshape_squeeze.6
  2.3 0.9 convert_element_type.9
  3.2 0.1 broadcast_in_dim.13
  3.3 0.7 pad_maximum_fusion
  4.0 18.5 %all_to_all.15 = f32[4,4,16384]{2,1,0:T(4,128)S(1)} all-to-all(f32[4,4,16384]{2,1,0:T(4,128)S(1)} %pad_maximum_fusion), channel_id=1, replica_groups=mesh['tm'=4,'lev'=8] {'tm'}, dimensions={0} | all-to-all | bytes 2097152 | tf_op jit(solution)/shard_map/all_to_all | solution.py:262
  22.5 4.4 %all-to-all-start.1 = ((f32[4,256,512]{2,1,0:T(8,128)}), f32[4,256,512]{2,1,0:T(8,128)}, u32[]{:S(2)}, u32[]{:S(2)}) async-start(f32[4,256,512]{2,1,0:T(8,128)} %bitcast.1), calls=%async_computation.1 | async-start | bytes 4194304 | tf_op jit(solution)/shard_map/all_to_all | solution.py:267
  27.0 1.2 fusion.1
  28.1 1.0 slice.21.innov_ref
  29.1 45.5 %shard_map.118.field_ref = f32[4,256,512]{2,1,0:T(8,128)} custom-call(s32[4,1,16384]{2,1,0:T(1,128)} %get-tuple-element.6.cell_ref, f32[4,2,16384]{2,1,0:T(2,128)} %slice.21.innov_ref), custom_call_target="tpu_custom_call" | custom-call | flops 34359738368 | bytes 8388608 | tf_op jit(solution)/shard_map/pallas_call | solution.py:88
  74.7 0.2 copy.33
  74.9 0.0 all-to-all-done.1.tangent_ref
  74.9 0.6 tile.11
  75.5 42.7 %shard_map.119 = f32[1024,128]{1,0:T(8,128)} custom-call(f32[4,256,512]{2,1,0:T(8,128)} %shard_map.118.field_ref, f32[4,256,512]{2,1,0:T(8,128)} %all-to-all-done.1.tangent_ref, f32[4,8,128]{2,1,0:T(8,128)} %bitcast.21, bf16[256,512]{1,0:T(8,128)(2,1)} %constant.33.clone.fhigh_ref, bf16[256,512]{1,0:T(8,128)(2,1)} %constant.34.clone.flow_ref, ...), custom_call_target="tpu_custom_call" | custom-call | tf_op jit(solution)/shard_map/pallas_call | solution.py:217
  118.2 1.1 slice.24
  119.3 0.4 reshape.43
  119.8 0.0 copy-start.1
  119.8 0.8 copy.28
  120.6 1.7 %reshape.46 = f32[32,2,1024]{2,1,0:T(2,128)} reshape(f32[8,4,2,16,2,32]{5,4,3,2,1,0:T(2,128)S(1)} %copy.28) | data formatting | bytes 524288 | tf_op jit(solution)/shard_map/reshape | solution.py:278
  122.3 6.3 %all-to-all-start.2 = ((f32[32,2,1024]{2,1,0:T(2,128)}), f32[32,2,1024]{2,1,0:T(2,128)S(1)}, u32[]{:S(2)}, u32[]{:S(2)}) async-start(f32[32,2,1024]{2,1,0:T(2,128)} %reshape.46), calls=%async_computation.2 | async-start | bytes 524288 | tf_op jit(solution)/shard_map/all_to_all | solution.py:279
  128.6 0.0 copy-done.1
  128.6 0.1 constant_dynamic-slice_fusion
  128.7 0.1 copy.25
  128.8 0.1 mul.19
  128.8 0.2 copy.26
  129.0 10.2 %all-to-all-done.2 = f32[32,2,1024]{2,1,0:T(2,128)S(1)} async-done(((f32[32,2,1024]{2,1,0:T(2,128)}), f32[32,2,1024]{2,1,0:T(2,128)S(1)}, u32[]{:S(2)}, u32[]{:S(2)}) %all-to-all-start.2) | async-done | bytes 262176 | tf_op jit(solution)/shard_map/all_to_all | solution.py:279
  139.2 0.2 reshape_reshape.3
  139.4 0.0 copy-done
  139.4 0.4 convolution_bitcast_fusion
  139.8 1.0 copy.27
  (6 shorter events, 0.1 us)
Async XLA Ops:
  0.0 139.4 %copy-start = (f32[64,64]{1,0:T(8,128)S(1)}, f32[64,64]{1,0:T(8,128)}, u32[]{:S(2)}) copy-start(f32[64,64]{1,0:T(8,128)} %param.17) | copy-start | bytes 49156
  22.5 52.3 %all-to-all-start.1 = ((f32[4,256,512]{2,1,0:T(8,128)}), f32[4,256,512]{2,1,0:T(8,128)}, u32[]{:S(2)}, u32[]{:S(2)}) async-start(f32[4,256,512]{2,1,0:T(8,128)} %bitcast.1), calls=%async_computation.1 | async-start | bytes 4194304 | tf_op jit(solution)/shard_map/all_to_all | solution.py:267
  119.8 8.9 %copy-start.1 = (f32[64,128]{1,0:T(8,128)S(1)}, f32[64,128]{1,0:T(8,128)}, u32[]{:S(2)}) copy-start(f32[64,128]{1,0:T(8,128)} %param.16) | copy-start | bytes 98308
  122.3 16.9 %all-to-all-start.2 = ((f32[32,2,1024]{2,1,0:T(2,128)}), f32[32,2,1024]{2,1,0:T(2,128)S(1)}, u32[]{:S(2)}, u32[]{:S(2)}) async-start(f32[32,2,1024]{2,1,0:T(2,128)} %reshape.46), calls=%async_computation.2 | async-start | bytes 524288 | tf_op jit(solution)/shard_map/all_to_all | solution.py:279
